TPU v7x, 32 devices: a whole 2x2x4 slice. The times are simulated.
32 devices in a mesh: dp: 4 (over z), feat: 8 (over y, x, core).
Axes of the slice: x: 2, y: 2, z: 4, core: 2. Of those that a mesh axis runs over, the one named last changes fastest.
Arguments:
- features: float32 [4096, 8192], P('dp', 'feat'), may hold values from -0.0625 to 0.0625
- labels: int32 [4096], P('dp'), may hold values from -1 to 1, as said below
- weights: float32 [8192], P('feat'), may hold values from -6 to 6
Outputs:
- gradient: float32 [8192], P('feat')
- newton_step: float32 [8192], P('feat')
- residual: float32 [8192], P('feat')
Inputs may be any that keep to these rules, and one draw needn't show every extreme that they name: `labels`: every label is -1 or +1.
All inputs are finite; a program needn't handle non-finite values.
Results may differ from a plain program's by a relative error of at most 0.0003.
Values sent between devices are 32-bit elements; how exact they have to be, the bound alone decides.
A program may use at most 64 MiB of HBM per device.

v0:
```python
import jax
import jax.numpy as jnp
from jax import lax
from jax.sharding import PartitionSpec as P

CG_STEPS = 3
PENALTY = 4.0
HIGH = lax.Precision.HIGHEST


def squares(residual):
    return lax.psum(jnp.sum(residual * residual), "feat")


def local(features, labels, weights):
    y = labels.astype(jnp.float32)
    margin = y * lax.psum(jnp.dot(features, weights, precision=HIGH), "feat")
    sig = 1.0 / (1.0 + jnp.exp(-margin))
    local_grad = jnp.dot((sig - 1.0) * y, features, precision=HIGH)
    gradient = weights + PENALTY * lax.psum(local_grad, "dp")
    curv = PENALTY * sig * (1.0 - sig)
    newton_step = jnp.zeros_like(weights)
    residual = -gradient
    direction = residual
    rr = squares(residual)
    for step in range(CG_STEPS):
        image_rows, dir_sq = lax.psum(
            (jnp.dot(features, direction, precision=HIGH), jnp.sum(direction * direction)), "feat"
        )
        weighted = curv * image_rows
        back, quad = lax.psum(
            (jnp.dot(weighted, features, precision=HIGH), jnp.sum(weighted * image_rows)), "dp"
        )
        curvature = dir_sq + quad
        image = direction + back
        alpha = rr / curvature
        newton_step = newton_step + alpha * direction
        residual = residual - alpha * image
        fresh = squares(residual)
        direction = residual + fresh / rr * direction
        rr = fresh
    return (gradient, newton_step, residual)


def solution(mesh):
    placed = (P("dp", "feat"), P("dp"), P("feat"))
    return jax.shard_map(
        local,
        mesh=mesh,
        in_specs=placed,
        out_specs=(P("feat"), P("feat"), P("feat")),
        check_vma=False,
    )
```

profile of v0, /device:TPU:0, one launch (start us, length us, event | category | flops | bytes accessed | tf_op | source)
XLA Modules:
  0.0 174.1 jit_solution(13997829717275814949)
XLA Ops:
  0.6 0.0 copy-start.2
  0.6 0.0 copy-start.1
  0.7 5.8 %fusion.3 = f32[1,1024]{1,0:T(1,128)S(1)} fusion(f32[1024,1024]{1,0:T(8,128)} %param.3, f32[1024,1]{0,1:T(1,128)} %bitcast.34), kind=kOutput, calls=%fused_computation.21 | convolution fusion | flops 12582912 | bytes 4202496 | tf_op jit(solution)/shard_map/dot_general | solution.py:17
  6.4 15.2 %psum.115 = f32[1024]{0:T(1024)S(1)} all-reduce(f32[1024]{0:T(1024)S(1)} %bitcast.45), channel_id=1, replica_groups=mesh['dp'=4,'feat'=8] {'feat'}, use_global_device_ids=true, to_apply=%region_0.0 | all-reduce | flops 1024 | bytes 8192 | tf_op jit(solution)/shard_map/psum | solution.py:17
  21.6 0.0 copy-done.2
  21.6 4.3 %fusion.4 = f32[1,1024]{1,0:T(1,128)S(1)} fusion(f32[1024,1]{0,1:T(1,128)S(1)} %bitcast.47, f32[1024,1024]{1,0:T(8,128)} %param.3), kind=kOutput, calls=%fused_computation.22 | convolution fusion | flops 12582912 | bytes 4202496 | tf_op jit(solution)/shard_map/dot_general | solution.py:19
  25.9 11.9 %psum.116 = f32[1024]{0:T(1024)S(1)} all-reduce(f32[1024]{0:T(1024)S(1)} %bitcast.44), channel_id=1, replica_groups=mesh['dp'=4,'feat'=8] {'dp'}, use_global_device_ids=true, to_apply=%region_1.0 | all-reduce | flops 1024 | bytes 8192 | tf_op jit(solution)/shard_map/psum | solution.py:20
  37.8 0.0 copy-done.1
  37.8 0.6 multiply_reduce_fusion.7
  38.4 5.6 %fusion.5 = f32[1,1024]{1,0:T(1,128)S(1)} fusion(f32[1024,1]{0,1:T(1,128)S(1)} %bitcast.46, f32[1024,1024]{1,0:T(8,128)} %param.3), kind=kOutput, calls=%fused_computation.23 | convolution fusion | flops 12582912 | bytes 4202496 | tf_op jit(solution)/shard_map/dot_general | solution.py:28
  44.1 12.8 %all-reduce.2 = (f32[1024]{0:T(1024)S(1)}, f32[]{:T(128)}) all-reduce(f32[1024]{0:T(1024)S(1)} %bitcast.38, f32[]{:T(128)} %get-tuple-element.21), channel_id=1, replica_groups=mesh['dp'=4,'feat'=8] {'feat'}, use_global_device_ids=true, to_apply=%region_4.0 | all-reduce | flops 1025 | bytes 8200 | tf_op jit(solution)/shard_map/psum | solution.py:27
  56.8 0.6 multiply_reduce_fusion.6
  57.4 4.3 %fusion.6 = f32[1,1024]{1,0:T(1,128)S(1)} fusion(f32[1024,1]{0,1:T(1,128)S(1)} %bitcast.36, f32[1024,1024]{1,0:T(8,128)} %param.3), kind=kOutput, calls=%fused_computation.24 | convolution fusion | flops 12582912 | bytes 4202496 | tf_op jit(solution)/shard_map/dot_general | solution.py:32
  61.7 9.1 %all-reduce.5 = (f32[1024]{0:T(1024)S(1)}, f32[]{:T(128)}) all-reduce(f32[1024]{0:T(1024)S(1)} %bitcast.39, f32[]{:T(128)} %get-tuple-element.29), channel_id=1, replica_groups=mesh['dp'=4,'feat'=8] {'dp'}, use_global_device_ids=true, to_apply=%region_7.0 | all-reduce | flops 1025 | bytes 8200 | tf_op jit(solution)/shard_map/psum | solution.py:31
  72.7 0.6 multiply_reduce_fusion.5
  73.3 12.6 %psum.121 = f32[]{:T(128)} all-reduce(f32[]{:T(128)} %multiply_reduce_fusion.5), channel_id=1, replica_groups=mesh['dp'=4,'feat'=8] {'feat'}, use_global_device_ids=true, to_apply=%region_9.0 | all-reduce | flops 1 | bytes 8 | tf_op jit(solution)/shard_map/psum | solution.py:12
  87.3 0.6 multiply_reduce_fusion.4
  87.9 5.6 %fusion.7 = f32[1,1024]{1,0:T(1,128)S(1)} fusion(f32[1024,1]{0,1:T(1,128)S(1)} %bitcast.32, f32[1024,1024]{1,0:T(8,128)} %param.3), kind=kOutput, calls=%fused_computation.25 | convolution fusion | flops 12582912 | bytes 4202496 | tf_op jit(solution)/shard_map/dot_general | solution.py:28
  93.5 12.8 %all-reduce.1 = (f32[1024]{0:T(1024)S(1)}, f32[]{:T(128)}) all-reduce(f32[1024]{0:T(1024)S(1)} %bitcast.42, f32[]{:T(128)} %get-tuple-element.19), channel_id=1, replica_groups=mesh['dp'=4,'feat'=8] {'feat'}, use_global_device_ids=true, to_apply=%region_12.0 | all-reduce | flops 1025 | bytes 8200 | tf_op jit(solution)/shard_map/psum | solution.py:27
  106.3 0.7 multiply_reduce_fusion.3
  107.0 4.3 %fusion.8 = f32[1,1024]{1,0:T(1,128)S(1)} fusion(f32[1024,1]{0,1:T(1,128)S(1)} %bitcast.37, f32[1024,1024]{1,0:T(8,128)} %param.3), kind=kOutput, calls=%fused_computation.26 | convolution fusion | flops 12582912 | bytes 4202496 | tf_op jit(solution)/shard_map/dot_general | solution.py:32
  111.2 11.1 %all-reduce.4 = (f32[1024]{0:T(1024)S(1)}, f32[]{:T(128)}) all-reduce(f32[1024]{0:T(1024)S(1)} %bitcast.40, f32[]{:T(128)} %get-tuple-element.27), channel_id=1, replica_groups=mesh['dp'=4,'feat'=8] {'dp'}, use_global_device_ids=true, to_apply=%region_15.0 | all-reduce | flops 1025 | bytes 8200 | tf_op jit(solution)/shard_map/psum | solution.py:31
  124.2 0.6 multiply_reduce_fusion.2
  124.8 12.4 %psum.126 = f32[]{:T(128)} all-reduce(f32[]{:T(128)} %get-tuple-element.17), channel_id=1, replica_groups=mesh['dp'=4,'feat'=8] {'feat'}, use_global_device_ids=true, to_apply=%region_17.0 | all-reduce | flops 1 | bytes 8 | tf_op jit(solution)/shard_map/psum | solution.py:12
  138.6 0.6 multiply_reduce_fusion.1
  139.2 5.6 %fusion.9 = f32[1,1024]{1,0:T(1,128)S(1)} fusion(f32[1024,1]{0,1:T(1,128)S(1)} %bitcast.33, f32[1024,1024]{1,0:T(8,128)} %param.3), kind=kOutput, calls=%fused_computation.27 | convolution fusion | flops 12582912 | bytes 4202496 | tf_op jit(solution)/shard_map/dot_general | solution.py:28
  144.8 12.7 %all-reduce = (f32[]{:T(128)}, f32[1024]{0:T(1024)S(1)}) all-reduce(f32[]{:T(128)} %get-tuple-element.15, f32[1024]{0:T(1024)S(1)} %bitcast.43), channel_id=1, replica_groups=mesh['dp'=4,'feat'=8] {'feat'}, use_global_device_ids=true, to_apply=%region_19.0 | all-reduce | flops 1025 | bytes 8200 | tf_op jit(solution)/shard_map/psum | solution.py:27
  157.6 0.7 fusion
  158.3 4.3 %fusion.10 = f32[1,1024]{1,0:T(1,128)S(1)} fusion(f32[1024,1]{0,1:T(1,128)S(1)} %bitcast.35, f32[1024,1024]{1,0:T(8,128)} %param.3), kind=kOutput, calls=%fused_computation.28 | convolution fusion | flops 12582912 | bytes 4202496 | tf_op jit(solution)/shard_map/dot_general | solution.py:32
  162.5 9.1 %all-reduce.3 = (f32[]{:T(128)}, f32[1024]{0:T(1024)S(1)}) all-reduce(f32[]{:T(128)} %get-tuple-element.26, f32[1024]{0:T(1024)S(1)} %bitcast.41), channel_id=1, replica_groups=mesh['dp'=4,'feat'=8] {'dp'}, use_global_device_ids=true, to_apply=%region_22.0 | all-reduce | flops 1025 | bytes 8200 | tf_op jit(solution)/shard_map/psum | solution.py:31
  173.5 0.0 copy-done
  173.5 0.6 multiply_subtract_fusion
  (3 shorter events, 0.0 us)
Async XLA Ops:
  0.6 20.9 %copy-start.2 = (s32[1024]{0:T(1024)S(1)}, s32[1024]{0:T(1024)}, u32[]{:S(2)}) copy-start(s32[1024]{0:T(1024)} %param.4) | copy-start | bytes 12292
  0.6 37.2 %copy-start.1 = (f32[1024]{0:T(1024)S(1)}, f32[1024]{0:T(1024)}, u32[]{:S(2)}) copy-start(f32[1024]{0:T(1024)} %param.5) | copy-start | bytes 12292
  38.4 135.1 %copy-start = (f32[1024]{0:T(1024)}, f32[1024]{0:T(1024)S(1)}, u32[]{:S(2)}) copy-start(f32[1024]{0:T(1024)S(1)} %get-tuple-element.22) | copy-start | bytes 12292
where the time goes:
time: 175 us; the launch traced here: 174 us
  blocking collectives  120 us (69%)
  matrix products  39.8 us (23%)
  between operations  9.03 us (5%)
  other arithmetic  5.6 us (3%)
    psum x3, blocking collectives, local(): lax.psum((jnp.dot(features, direction, precision=HIGH), jnp.sum(direction...  38.2 us
    psum x3, blocking collectives, local(): lax.psum((jnp.dot(weighted, features, precision=HIGH), jnp.sum(weighted *...  29.4 us
    psum x2, blocking collectives, squares(): return lax.psum(jnp.sum(residual * residual), 'feat')  25 us
    dot_general x3, matrix products, local(): jnp.dot(features, direction, precision=HIGH)  16.9 us
    psum x1, blocking collectives, local(): margin = y * lax.psum(jnp.dot(features, weights, precision=HIGH), 'feat')  15.2 us
    dot_general x3, matrix products, local(): jnp.dot(weighted, features, precision=HIGH)  12.8 us
    psum x1, blocking collectives, local(): gradient = weights + PENALTY * lax.psum(local_grad, 'dp')  11.9 us
    dot_general x1, matrix products, local(): margin = y * lax.psum(jnp.dot(features, weights, precision=HIGH), 'feat')  5.76 us

commit v1 on v0

--- a/solution.py
+++ b/solution.py
@@ -14,7 +14,7 @@
 
 def local(features, labels, weights):
     y = labels.astype(jnp.float32)
-    margin = y * lax.psum(jnp.dot(features, weights, precision=HIGH), "feat")
+    margin = y * jnp.sum(lax.all_gather(jnp.dot(features, weights, precision=HIGH), "feat"), axis=0)
     sig = 1.0 / (1.0 + jnp.exp(-margin))
     local_grad = jnp.dot((sig - 1.0) * y, features, precision=HIGH)
     gradient = weights + PENALTY * lax.psum(local_grad, "dp")

time: 175 us -> 170 us (0.971)
  blocking collectives: 120 us -> 115 us
    psum x1 -> x0, blocking collectives: 15.2 us -> none  [local(): margin = y * lax.psum(jnp.dot(features, weights, precision=HIGH), 'feat')]
    all_gather x0 -> x1, blocking collectives: none -> 10.6 us  [local(): lax.all_gather(jnp.dot(features, weights, precision=HIGH), 'feat')]
where the time goes in v1:
time: 170 us; the launch traced here: 169 us
  blocking collectives  115 us (68%)
  matrix products  39.8 us (23%)
  between operations  9.04 us (5%)
  other arithmetic  5.62 us (3%)
    psum x3, blocking collectives, local(): lax.psum((jnp.dot(features, direction, precision=HIGH), jnp.sum(direction...  38.1 us
    psum x3, blocking collectives, local(): lax.psum((jnp.dot(weighted, features, precision=HIGH), jnp.sum(weighted *...  29.4 us
    psum x2, blocking collectives, squares(): return lax.psum(jnp.sum(residual * residual), 'feat')  25 us
    dot_general x3, matrix products, local(): jnp.dot(features, direction, precision=HIGH)  16.9 us
    dot_general x3, matrix products, local(): jnp.dot(weighted, features, precision=HIGH)  12.8 us
    psum x1, blocking collectives, local(): gradient = weights + PENALTY * lax.psum(local_grad, 'dp')  11.9 us
    all_gather x1, blocking collectives, local(): lax.all_gather(jnp.dot(features, weights, precision=HIGH), 'feat')  10.6 us
    dot_general x1, matrix products, local(): jnp.dot(features, weights, precision=HIGH)  5.76 us

profile of v1, /device:TPU:0, one launch (start us, length us, event | category | flops | bytes accessed | tf_op | source)
XLA Modules:
  0.0 169.4 jit_solution(1365845633718539054)
XLA Ops:
  0.6 0.0 copy-start.2
  0.6 0.0 copy-start.1
  0.7 5.8 %fusion.3 = f32[1,1024]{1,0:T(1,128)S(1)} fusion(f32[1024,1024]{1,0:T(8,128)} %param.3, f32[1024,1]{0,1:T(1,128)} %bitcast.34), kind=kOutput, calls=%fused_computation.21 | convolution fusion | flops 12582912 | bytes 4202496 | tf_op jit(solution)/shard_map/dot_general | solution.py:17
  6.4 10.6 %all-gather = f32[8192]{0:T(1024)S(1)} all-gather(f32[1024]{0:T(1024)S(1)} %bitcast.38), channel_id=2, replica_groups=mesh['dp'=4,'feat'=8] {'feat'}, dimensions={0}, use_global_device_ids=true | all-gather | bytes 36864 | tf_op jit(solution)/shard_map/all_gather | solution.py:17
  17.0 0.0 copy-done.2
  17.1 4.3 %fusion.4 = f32[1,1024]{1,0:T(1,128)S(1)} fusion(f32[1024,1]{0,1:T(1,128)S(1)} %bitcast.47, f32[1024,1024]{1,0:T(8,128)} %param.3), kind=kOutput, calls=%fused_computation.22 | convolution fusion | flops 12582912 | bytes 4202496 | tf_op jit(solution)/shard_map/dot_general | solution.py:19
  21.3 11.9 %psum.108 = f32[1024]{0:T(1024)S(1)} all-reduce(f32[1024]{0:T(1024)S(1)} %bitcast.45), channel_id=1, replica_groups=mesh['dp'=4,'feat'=8] {'dp'}, use_global_device_ids=true, to_apply=%region_1.0 | all-reduce | flops 1024 | bytes 8192 | tf_op jit(solution)/shard_map/psum | solution.py:20
  33.3 0.0 copy-done.1
  33.3 0.6 multiply_reduce_fusion.7
  33.9 5.6 %fusion.5 = f32[1,1024]{1,0:T(1,128)S(1)} fusion(f32[1024,1]{0,1:T(1,128)S(1)} %bitcast.46, f32[1024,1024]{1,0:T(8,128)} %param.3), kind=kOutput, calls=%fused_computation.23 | convolution fusion | flops 12582912 | bytes 4202496 | tf_op jit(solution)/shard_map/dot_general | solution.py:28
  39.5 12.7 %all-reduce.2 = (f32[1024]{0:T(1024)S(1)}, f32[]{:T(128)}) all-reduce(f32[1024]{0:T(1024)S(1)} %bitcast.39, f32[]{:T(128)} %get-tuple-element.21), channel_id=1, replica_groups=mesh['dp'=4,'feat'=8] {'feat'}, use_global_device_ids=true, to_apply=%region_4.0 | all-reduce | flops 1025 | bytes 8200 | tf_op jit(solution)/shard_map/psum | solution.py:27
  52.3 0.6 multiply_reduce_fusion.6
  52.9 4.3 %fusion.6 = f32[1,1024]{1,0:T(1,128)S(1)} fusion(f32[1024,1]{0,1:T(1,128)S(1)} %bitcast.36, f32[1024,1024]{1,0:T(8,128)} %param.3), kind=kOutput, calls=%fused_computation.24 | convolution fusion | flops 12582912 | bytes 4202496 | tf_op jit(solution)/shard_map/dot_general | solution.py:32
  57.2 9.1 %all-reduce.5 = (f32[1024]{0:T(1024)S(1)}, f32[]{:T(128)}) all-reduce(f32[1024]{0:T(1024)S(1)} %bitcast.40, f32[]{:T(128)} %get-tuple-element.29), channel_id=1, replica_groups=mesh['dp'=4,'feat'=8] {'dp'}, use_global_device_ids=true, to_apply=%region_7.0 | all-reduce | flops 1025 | bytes 8200 | tf_op jit(solution)/shard_map/psum | solution.py:31
  68.2 0.6 multiply_reduce_fusion.5
  68.8 12.6 %psum.113 = f32[]{:T(128)} all-reduce(f32[]{:T(128)} %multiply_reduce_fusion.5), channel_id=1, replica_groups=mesh['dp'=4,'feat'=8] {'feat'}, use_global_device_ids=true, to_apply=%region_9.0 | all-reduce | flops 1 | bytes 8 | tf_op jit(solution)/shard_map/psum | solution.py:12
  82.8 0.6 multiply_reduce_fusion.4
  83.4 5.6 %fusion.7 = f32[1,1024]{1,0:T(1,128)S(1)} fusion(f32[1024,1]{0,1:T(1,128)S(1)} %bitcast.32, f32[1024,1024]{1,0:T(8,128)} %param.3), kind=kOutput, calls=%fused_computation.25 | convolution fusion | flops 12582912 | bytes 4202496 | tf_op jit(solution)/shard_map/dot_general | solution.py:28
  89.0 12.7 %all-reduce.1 = (f32[1024]{0:T(1024)S(1)}, f32[]{:T(128)}) all-reduce(f32[1024]{0:T(1024)S(1)} %bitcast.43, f32[]{:T(128)} %get-tuple-element.19), channel_id=1, replica_groups=mesh['dp'=4,'feat'=8] {'feat'}, use_global_device_ids=true, to_apply=%region_12.0 | all-reduce | flops 1025 | bytes 8200 | tf_op jit(solution)/shard_map/psum | solution.py:27
  101.7 0.7 multiply_reduce_fusion.3
  102.4 4.3 %fusion.8 = f32[1,1024]{1,0:T(1,128)S(1)} fusion(f32[1024,1]{0,1:T(1,128)S(1)} %bitcast.37, f32[1024,1024]{1,0:T(8,128)} %param.3), kind=kOutput, calls=%fused_computation.26 | convolution fusion | flops 12582912 | bytes 4202496 | tf_op jit(solution)/shard_map/dot_general | solution.py:32
  106.6 11.1 %all-reduce.4 = (f32[1024]{0:T(1024)S(1)}, f32[]{:T(128)}) all-reduce(f32[1024]{0:T(1024)S(1)} %bitcast.41, f32[]{:T(128)} %get-tuple-element.27), channel_id=1, replica_groups=mesh['dp'=4,'feat'=8] {'dp'}, use_global_device_ids=true, to_apply=%region_15.0 | all-reduce | flops 1025 | bytes 8200 | tf_op jit(solution)/shard_map/psum | solution.py:31
  119.6 0.6 multiply_reduce_fusion.2
  120.2 12.4 %psum.118 = f32[]{:T(128)} all-reduce(f32[]{:T(128)} %get-tuple-element.17), channel_id=1, replica_groups=mesh['dp'=4,'feat'=8] {'feat'}, use_global_device_ids=true, to_apply=%region_17.0 | all-reduce | flops 1 | bytes 8 | tf_op jit(solution)/shard_map/psum | solution.py:12
  134.0 0.6 multiply_reduce_fusion.1
  134.6 5.6 %fusion.9 = f32[1,1024]{1,0:T(1,128)S(1)} fusion(f32[1024,1]{0,1:T(1,128)S(1)} %bitcast.33, f32[1024,1024]{1,0:T(8,128)} %param.3), kind=kOutput, calls=%fused_computation.27 | convolution fusion | flops 12582912 | bytes 4202496 | tf_op jit(solution)/shard_map/dot_general | solution.py:28
  140.2 12.7 %all-reduce = (f32[]{:T(128)}, f32[1024]{0:T(1024)S(1)}) all-reduce(f32[]{:T(128)} %get-tuple-element.15, f32[1024]{0:T(1024)S(1)} %bitcast.44), channel_id=1, replica_groups=mesh['dp'=4,'feat'=8] {'feat'}, use_global_device_ids=true, to_apply=%region_19.0 | all-reduce | flops 1025 | bytes 8200 | tf_op jit(solution)/shard_map/psum | solution.py:27
  152.9 0.7 fusion
  153.6 4.3 %fusion.10 = f32[1,1024]{1,0:T(1,128)S(1)} fusion(f32[1024,1]{0,1:T(1,128)S(1)} %bitcast.35, f32[1024,1024]{1,0:T(8,128)} %param.3), kind=kOutput, calls=%fused_computation.28 | convolution fusion | flops 12582912 | bytes 4202496 | tf_op jit(solution)/shard_map/dot_general | solution.py:32
  157.9 9.1 %all-reduce.3 = (f32[]{:T(128)}, f32[1024]{0:T(1024)S(1)}) all-reduce(f32[]{:T(128)} %get-tuple-element.26, f32[1024]{0:T(1024)S(1)} %bitcast.42), channel_id=1, replica_groups=mesh['dp'=4,'feat'=8] {'dp'}, use_global_device_ids=true, to_apply=%region_22.0 | all-reduce | flops 1025 | bytes 8200 | tf_op jit(solution)/shard_map/psum | solution.py:31
  168.8 0.0 copy-done
  168.8 0.6 multiply_subtract_fusion
  (5 shorter events, 0.0 us)
Async XLA Ops:
  0.6 16.4 %copy-start.2 = (s32[1024]{0:T(1024)S(1)}, s32[1024]{0:T(1024)}, u32[]{:S(2)}) copy-start(s32[1024]{0:T(1024)} %param.4) | copy-start | bytes 12292
  0.6 32.6 %copy-start.1 = (f32[1024]{0:T(1024)S(1)}, f32[1024]{0:T(1024)}, u32[]{:S(2)}) copy-start(f32[1024]{0:T(1024)} %param.5) | copy-start | bytes 12292
  33.9 134.9 %copy-start = (f32[1024]{0:T(1024)}, f32[1024]{0:T(1024)S(1)}, u32[]{:S(2)}) copy-start(f32[1024]{0:T(1024)S(1)} %get-tuple-element.22) | copy-start | bytes 12292
